TPU v7x, 32 devices: a whole 2x2x4 slice. The times are simulated.
32 devices in a mesh: row: 8 (over z, y), col: 4 (over x, core).
Axes of the slice: x: 2, y: 2, z: 4, core: 2. Of those that a mesh axis runs over, the one named last changes fastest.
Arguments:
- root_rhs: bfloat16 [8, 8192], replicated, may hold values from -6 to 6
- diag_inv: bfloat16 [16, 512, 512], replicated, may hold values from -1 to 2
- tile_u: bfloat16 [8, 4, 2, 4, 128, 512], P('row', 'col'), may hold values from -0.1875 to 0.1875
- tile_v: bfloat16 [8, 4, 2, 4, 512, 128], P('row', 'col'), may hold values from -0.25 to 0.25
- tile_rank: int32 [8, 4, 2, 4], P('row', 'col'), may hold values from 16 to 128
- child_x: bfloat16 [32, 8, 512], P(('row', 'col')), may hold values from -6 to 6
- border_t: bfloat16 [32, 512, 1024], P(('row', 'col')), may hold values from -0.09375 to 0.09375
- child_inv: bfloat16 [32, 512, 512], P(('row', 'col')), may hold values from -1 to 2
- child_blocks: int32 [32, 8], P(('row', 'col')), may hold values from 0 to 63
Outputs:
- root_solution: float32 [8, 8192], P(None, ('row', 'col'))
- child_out: float32 [32, 8, 512], P(('row', 'col'))
All inputs are finite; a program needn't handle non-finite values.
Results may differ from a plain program's by a relative error of at most 0.017.
Values sent between devices are 32-bit elements; how exact they have to be, the bound alone decides.
A program may use at most 64 MiB of HBM per device.

v0:
```python
import jax
import jax.numpy as jnp
from jax import lax
from jax.sharding import PartitionSpec as P

BLK = 128
BB = 8


def per_device(
    root_rhs, diag_inv, tile_u, tile_v, tile_rank, child_x, border_t, child_inv, child_blocks
):
    highest_precision = lax.Precision.HIGHEST
    n_row = lax.axis_size("row")
    n_col = lax.axis_size("col")
    my_row = lax.axis_index("row")
    my_col = lax.axis_index("col")
    ntile = diag_inv.shape[0]
    tile = diag_inv.shape[1]
    rhs_count = root_rhs.shape[0]
    rank_max = tile_u.shape[4]
    t_rows = tile_u.shape[2]
    t_cols = tile_u.shape[3]
    left_tiles = tile_u[0, 0]
    right_tiles = tile_v[0, 0]
    tile_ranks = tile_rank[0, 0]
    blocks_per_front = tile // BLK
    n_child = child_x.shape[0]
    upward = jnp.einsum("crs,csb->crb", child_x, border_t, preferred_element_type=jnp.float32)
    pieces = (
        upward.reshape(n_child, rhs_count, BB, BLK)
        .transpose(1, 0, 2, 3)
        .reshape(rhs_count, n_child * BB, BLK)
    )
    flat_blocks = child_blocks.reshape(-1)
    dense_sum = (
        jnp.zeros((rhs_count, ntile * blocks_per_front, BLK), jnp.float32)
        .at[:, flat_blocks, :]
        .add(pieces)
    )
    dense_sum = dense_sum.reshape(rhs_count, ntile, tile)
    right_side = root_rhs.reshape(rhs_count, ntile, tile)
    col_ids = my_col + n_col * jnp.arange(t_cols)
    row_ids = my_row + n_row * jnp.arange(t_rows)
    rank_iota = jnp.arange(rank_max)

    def forward(column, solved_rows):
        owner_slot = column // n_row
        on_row = column % n_row == my_row
        known_cols = jnp.take(solved_rows, col_ids, axis=1).astype(jnp.bfloat16)
        right_row = lax.dynamic_index_in_dim(right_tiles, owner_slot, 0, keepdims=False)
        left_row_index = lax.dynamic_index_in_dim(left_tiles, owner_slot, 0, keepdims=False)
        rank_row = lax.dynamic_index_in_dim(tile_ranks, owner_slot, 0, keepdims=False)
        live_mask = (rank_iota[None, :] < rank_row[:, None]) & (col_ids[:, None] < column) & on_row
        coefficient_values = jnp.einsum(
            "rbt,btq->rbq", known_cols, right_row, preferred_element_type=jnp.float32
        )
        coefficient_values = jnp.where(live_mask[None], coefficient_values, 0.0).astype(
            jnp.bfloat16
        )
        partial_value = jnp.einsum(
            "rbq,bqt->rt", coefficient_values, left_row_index, preferred_element_type=jnp.float32
        )
        carried = lax.dynamic_index_in_dim(dense_sum, column, 1, keepdims=False)
        row_total = lax.psum(partial_value + carried, ("row", "col"))
        block_rhs = lax.dynamic_index_in_dim(right_side, column, 1, keepdims=False).astype(
            jnp.float32
        )
        inverse = lax.dynamic_index_in_dim(diag_inv, column, 0, keepdims=False).astype(jnp.float32)
        fresh = jnp.dot(block_rhs - row_total, inverse, precision=highest_precision)
        return lax.dynamic_update_index_in_dim(solved_rows, fresh, column, 1)

    solved_rows = lax.fori_loop(0, ntile, forward, jnp.zeros((rhs_count, ntile, tile), jnp.float32))

    def backward(sweep, result):
        column = ntile - 1 - sweep
        owner_slot = column // n_col
        on_col = column % n_col == my_col
        known_rows = jnp.take(result, row_ids, axis=1).astype(jnp.bfloat16)
        left_col = lax.dynamic_index_in_dim(left_tiles, owner_slot, 1, keepdims=False)
        right_col = lax.dynamic_index_in_dim(right_tiles, owner_slot, 1, keepdims=False)
        rank_col = lax.dynamic_index_in_dim(tile_ranks, owner_slot, 1, keepdims=False)
        live_mask = (rank_iota[None, :] < rank_col[:, None]) & (row_ids[:, None] > column) & on_col
        coefficient_values = jnp.einsum(
            "rat,aqt->raq", known_rows, left_col, preferred_element_type=jnp.float32
        )
        coefficient_values = jnp.where(live_mask[None], coefficient_values, 0.0).astype(
            jnp.bfloat16
        )
        partial_value = jnp.einsum(
            "raq,atq->rt", coefficient_values, right_col, preferred_element_type=jnp.float32
        )
        col_total = lax.psum(partial_value, ("row", "col"))
        block_solved = lax.dynamic_index_in_dim(solved_rows, column, 1, keepdims=False)
        inverse = lax.dynamic_index_in_dim(diag_inv, column, 0, keepdims=False).astype(jnp.float32)
        fresh = jnp.dot(block_solved - col_total, inverse.T, precision=highest_precision)
        return lax.dynamic_update_index_in_dim(result, fresh, column, 1)

    result = lax.fori_loop(0, ntile, backward, jnp.zeros((rhs_count, ntile, tile), jnp.float32))
    share = ntile * tile // (n_row * n_col)
    start = (my_row * n_col + my_col) * share
    root_part = lax.dynamic_slice_in_dim(result.reshape(rhs_count, ntile * tile), start, share, 1)
    gathered = result.reshape(rhs_count, ntile * blocks_per_front, BLK)[:, flat_blocks, :]
    gathered = gathered.reshape(rhs_count, n_child, BB * BLK).astype(jnp.bfloat16)
    returned = jnp.einsum("rcb,csb->crs", gathered, border_t, preferred_element_type=jnp.float32)
    child_out = child_x.astype(jnp.float32) - jnp.einsum(
        "crs,cst->crt", returned, child_inv.astype(jnp.float32), precision=highest_precision
    )
    return (root_part, child_out)


def solution(mesh):
    return jax.shard_map(
        per_device,
        mesh=mesh,
        in_specs=(
            P(),
            P(),
            P("row", "col", None, None, None, None),
            P("row", "col", None, None, None, None),
            P("row", "col", None, None),
            P(("row", "col"), None, None),
            P(("row", "col"), None, None),
            P(("row", "col"), None, None),
            P(("row", "col"), None),
        ),
        out_specs=(P(None, ("row", "col")), P(("row", "col"), None, None)),
        check_vma=False,
    )
```

profile of v0, /device:TPU:0, one launch (start us, length us, event | category | flops | bytes accessed | tf_op | source)
XLA Modules:
  0.0 1424.4 jit_solution(4886888711580385367)
XLA Ops:
  5.8 715.2 %while.32 = (s32[]{:T(128)}, f32[8,16,512]{2,0,1:T(8,128)S(1)}, bf16[8,16,512]{2,1,0:T(8,128)(2,1)S(1)}, s32[2,4]{1,0:T(2,128)}, s32[]{:T(128)}, /*index=5*/bf16...) while((s32[]{:T(128)}, f32[8,16,512]{2,0,1:T(8,128)S(1)}, ...), condition=%wide.region_3.4_spmd.clone, body=%wide.region_1.3_spmd.clone.sunk | while | flops 33598024 | bytes 1818560 | solution.py:73
  9.0 42.0 %psum.32 = f32[8,512]{1,0:T(8,128)S(1)} all-reduce(f32[8,512]{1,0:T(8,128)S(1)} %fusion.106), channel_id=1, replica_groups=mesh['row'=8,'col'=4] {'row','col'}, use_global_device_ids=true, to_apply=%region_2.2 | all-reduce | flops 4096 | bytes 32768 | tf_op jit(solution)/shard_map/while/body/eval_jaxpr/psum | solution.py:65
  55.5 40.2 %psum.32 = f32[8,512]{1,0:T(8,128)S(1)} all-reduce(f32[8,512]{1,0:T(8,128)S(1)} %fusion.106), channel_id=1, replica_groups=mesh['row'=8,'col'=4] {'row','col'}, use_global_device_ids=true, to_apply=%region_2.2 | all-reduce | flops 4096 | bytes 32768 | tf_op jit(solution)/shard_map/while/body/eval_jaxpr/psum | solution.py:65
  100.2 40.0 %psum.32 = f32[8,512]{1,0:T(8,128)S(1)} all-reduce(f32[8,512]{1,0:T(8,128)S(1)} %fusion.106), channel_id=1, replica_groups=mesh['row'=8,'col'=4] {'row','col'}, use_global_device_ids=true, to_apply=%region_2.2 | all-reduce | flops 4096 | bytes 32768 | tf_op jit(solution)/shard_map/while/body/eval_jaxpr/psum | solution.py:65
  144.7 40.2 %psum.32 = f32[8,512]{1,0:T(8,128)S(1)} all-reduce(f32[8,512]{1,0:T(8,128)S(1)} %fusion.106), channel_id=1, replica_groups=mesh['row'=8,'col'=4] {'row','col'}, use_global_device_ids=true, to_apply=%region_2.2 | all-reduce | flops 4096 | bytes 32768 | tf_op jit(solution)/shard_map/while/body/eval_jaxpr/psum | solution.py:65
  189.4 39.9 %psum.32 = f32[8,512]{1,0:T(8,128)S(1)} all-reduce(f32[8,512]{1,0:T(8,128)S(1)} %fusion.106), channel_id=1, replica_groups=mesh['row'=8,'col'=4] {'row','col'}, use_global_device_ids=true, to_apply=%region_2.2 | all-reduce | flops 4096 | bytes 32768 | tf_op jit(solution)/shard_map/while/body/eval_jaxpr/psum | solution.py:65
  233.8 40.1 %psum.32 = f32[8,512]{1,0:T(8,128)S(1)} all-reduce(f32[8,512]{1,0:T(8,128)S(1)} %fusion.106), channel_id=1, replica_groups=mesh['row'=8,'col'=4] {'row','col'}, use_global_device_ids=true, to_apply=%region_2.2 | all-reduce | flops 4096 | bytes 32768 | tf_op jit(solution)/shard_map/while/body/eval_jaxpr/psum | solution.py:65
  278.5 40.0 %psum.32 = f32[8,512]{1,0:T(8,128)S(1)} all-reduce(f32[8,512]{1,0:T(8,128)S(1)} %fusion.106), channel_id=1, replica_groups=mesh['row'=8,'col'=4] {'row','col'}, use_global_device_ids=true, to_apply=%region_2.2 | all-reduce | flops 4096 | bytes 32768 | tf_op jit(solution)/shard_map/while/body/eval_jaxpr/psum | solution.py:65
  323.0 40.2 %psum.32 = f32[8,512]{1,0:T(8,128)S(1)} all-reduce(f32[8,512]{1,0:T(8,128)S(1)} %fusion.106), channel_id=1, replica_groups=mesh['row'=8,'col'=4] {'row','col'}, use_global_device_ids=true, to_apply=%region_2.2 | all-reduce | flops 4096 | bytes 32768 | tf_op jit(solution)/shard_map/while/body/eval_jaxpr/psum | solution.py:65
  367.7 39.8 %psum.32 = f32[8,512]{1,0:T(8,128)S(1)} all-reduce(f32[8,512]{1,0:T(8,128)S(1)} %fusion.106), channel_id=1, replica_groups=mesh['row'=8,'col'=4] {'row','col'}, use_global_device_ids=true, to_apply=%region_2.2 | all-reduce | flops 4096 | bytes 32768 | tf_op jit(solution)/shard_map/while/body/eval_jaxpr/psum | solution.py:65
  412.0 40.2 %psum.32 = f32[8,512]{1,0:T(8,128)S(1)} all-reduce(f32[8,512]{1,0:T(8,128)S(1)} %fusion.106), channel_id=1, replica_groups=mesh['row'=8,'col'=4] {'row','col'}, use_global_device_ids=true, to_apply=%region_2.2 | all-reduce | flops 4096 | bytes 32768 | tf_op jit(solution)/shard_map/while/body/eval_jaxpr/psum | solution.py:65
  456.7 39.8 %psum.32 = f32[8,512]{1,0:T(8,128)S(1)} all-reduce(f32[8,512]{1,0:T(8,128)S(1)} %fusion.106), channel_id=1, replica_groups=mesh['row'=8,'col'=4] {'row','col'}, use_global_device_ids=true, to_apply=%region_2.2 | all-reduce | flops 4096 | bytes 32768 | tf_op jit(solution)/shard_map/while/body/eval_jaxpr/psum | solution.py:65
  501.1 40.2 %psum.32 = f32[8,512]{1,0:T(8,128)S(1)} all-reduce(f32[8,512]{1,0:T(8,128)S(1)} %fusion.106), channel_id=1, replica_groups=mesh['row'=8,'col'=4] {'row','col'}, use_global_device_ids=true, to_apply=%region_2.2 | all-reduce | flops 4096 | bytes 32768 | tf_op jit(solution)/shard_map/while/body/eval_jaxpr/psum | solution.py:65
  590.1 40.3 %psum.32 = f32[8,512]{1,0:T(8,128)S(1)} all-reduce(f32[8,512]{1,0:T(8,128)S(1)} %fusion.106), channel_id=1, replica_groups=mesh['row'=8,'col'=4] {'row','col'}, use_global_device_ids=true, to_apply=%region_2.2 | all-reduce | flops 4096 | bytes 32768 | tf_op jit(solution)/shard_map/while/body/eval_jaxpr/psum | solution.py:65
  679.2 40.4 %psum.32 = f32[8,512]{1,0:T(8,128)S(1)} all-reduce(f32[8,512]{1,0:T(8,128)S(1)} %fusion.106), channel_id=1, replica_groups=mesh['row'=8,'col'=4] {'row','col'}, use_global_device_ids=true, to_apply=%region_2.2 | all-reduce | flops 4096 | bytes 32768 | tf_op jit(solution)/shard_map/while/body/eval_jaxpr/psum | solution.py:65
  721.8 700.1 %while.33 = (s32[]{:T(128)}, f32[8,16,512]{2,0,1:T(8,128)S(1)}, f32[8,16,512]{2,0,1:T(8,128)S(1)}, s32[2,4]{0,1:T(4,128)S(1)}, s32[]{:T(128)}, /*index=5*/bf16[2...) while((s32[]{:T(128)}, f32[8,16,512]{2,0,1:T(8,128)S(1)}, ...), condition=%wide.region_6.7_spmd.clone, body=%wide.region_4.6_spmd.clone.sunk | while | flops 29382456 | bytes 1203697 | solution.py:99
  767.2 40.5 %psum.33 = f32[8,512]{1,0:T(8,128)S(1)} all-reduce(f32[8,512]{1,0:T(8,128)S(1)} %fusion.113), channel_id=1, replica_groups=mesh['row'=8,'col'=4] {'row','col'}, use_global_device_ids=true, to_apply=%region_5.5 | all-reduce | flops 4096 | bytes 32768 | tf_op jit(solution)/shard_map/while/body/eval_jaxpr/psum | solution.py:93
  854.7 40.6 %psum.33 = f32[8,512]{1,0:T(8,128)S(1)} all-reduce(f32[8,512]{1,0:T(8,128)S(1)} %fusion.113), channel_id=1, replica_groups=mesh['row'=8,'col'=4] {'row','col'}, use_global_device_ids=true, to_apply=%region_5.5 | all-reduce | flops 4096 | bytes 32768 | tf_op jit(solution)/shard_map/while/body/eval_jaxpr/psum | solution.py:93
  942.1 40.7 %psum.33 = f32[8,512]{1,0:T(8,128)S(1)} all-reduce(f32[8,512]{1,0:T(8,128)S(1)} %fusion.113), channel_id=1, replica_groups=mesh['row'=8,'col'=4] {'row','col'}, use_global_device_ids=true, to_apply=%region_5.5 | all-reduce | flops 4096 | bytes 32768 | tf_op jit(solution)/shard_map/while/body/eval_jaxpr/psum | solution.py:93
  1029.6 40.7 %psum.33 = f32[8,512]{1,0:T(8,128)S(1)} all-reduce(f32[8,512]{1,0:T(8,128)S(1)} %fusion.113), channel_id=1, replica_groups=mesh['row'=8,'col'=4] {'row','col'}, use_global_device_ids=true, to_apply=%region_5.5 | all-reduce | flops 4096 | bytes 32768 | tf_op jit(solution)/shard_map/while/body/eval_jaxpr/psum | solution.py:93
  1117.1 40.7 %psum.33 = f32[8,512]{1,0:T(8,128)S(1)} all-reduce(f32[8,512]{1,0:T(8,128)S(1)} %fusion.113), channel_id=1, replica_groups=mesh['row'=8,'col'=4] {'row','col'}, use_global_device_ids=true, to_apply=%region_5.5 | all-reduce | flops 4096 | bytes 32768 | tf_op jit(solution)/shard_map/while/body/eval_jaxpr/psum | solution.py:93
  1204.6 40.7 %psum.33 = f32[8,512]{1,0:T(8,128)S(1)} all-reduce(f32[8,512]{1,0:T(8,128)S(1)} %fusion.113), channel_id=1, replica_groups=mesh['row'=8,'col'=4] {'row','col'}, use_global_device_ids=true, to_apply=%region_5.5 | all-reduce | flops 4096 | bytes 32768 | tf_op jit(solution)/shard_map/while/body/eval_jaxpr/psum | solution.py:93
  1292.2 40.7 %psum.33 = f32[8,512]{1,0:T(8,128)S(1)} all-reduce(f32[8,512]{1,0:T(8,128)S(1)} %fusion.113), channel_id=1, replica_groups=mesh['row'=8,'col'=4] {'row','col'}, use_global_device_ids=true, to_apply=%region_5.5 | all-reduce | flops 4096 | bytes 32768 | tf_op jit(solution)/shard_map/while/body/eval_jaxpr/psum | solution.py:93
  1379.7 40.7 %psum.33 = f32[8,512]{1,0:T(8,128)S(1)} all-reduce(f32[8,512]{1,0:T(8,128)S(1)} %fusion.113), channel_id=1, replica_groups=mesh['row'=8,'col'=4] {'row','col'}, use_global_device_ids=true, to_apply=%region_5.5 | all-reduce | flops 4096 | bytes 32768 | tf_op jit(solution)/shard_map/while/body/eval_jaxpr/psum | solution.py:93
  (286 shorter events, 533.8 us)
Async XLA Ops:
  0.6 1422.8 %copy-start = (bf16[1,512,512]{2,1,0:T(8,128)(2,1)S(1)}, bf16[1,512,512]{2,1,0:T(8,128)(2,1)}, u32[]{:S(2)}) copy-start(bf16[1,512,512]{2,1,0:T(8,128)(2,1)} %param.20) | copy-start | bytes 1572868
  5.7 1417.3 %copy-start.1 = (bf16[1,512,1024]{2,1,0:T(8,128)(2,1)S(1)}, bf16[1,512,1024]{2,1,0:T(8,128)(2,1)}, u32[]{:S(2)}) copy-start(bf16[1,512,1024]{2,1,0:T(8,128)(2,1)} %param.19) | copy-start | bytes 3145732
  5.8 1417.7 %copy-start.2 = (bf16[1,8,512]{2,1,0:T(8,128)(2,1)S(1)}, bf16[1,8,512]{2,1,0:T(8,128)(2,1)}, u32[]{:S(2)}) copy-start(bf16[1,8,512]{2,1,0:T(8,128)(2,1)} %param.18) | copy-start | bytes 24580
where the time goes:
time: 1430 us; the launch traced here: 1420 us
  blocking collectives  1280 us (90%)
  matrix products  100 us (7%)
  local copies, waits for them, and re-layouts  33.4 us (2%)
    psum x16, blocking collectives, forward(): row_total = lax.psum(partial_value + carried, ('row', 'col'))  643 us
    psum x16, blocking collectives, backward(): col_total = lax.psum(partial_value, ('row', 'col'))  641 us

commit v1 on v0

--- a/solution.py
+++ b/solution.py
@@ -62,7 +62,7 @@
             "rbq,bqt->rt", coefficient_values, left_row_index, preferred_element_type=jnp.float32
         )
         carried = lax.dynamic_index_in_dim(dense_sum, column, 1, keepdims=False)
-        row_total = lax.psum(partial_value + carried, ("row", "col"))
+        row_total = lax.psum(lax.psum(partial_value + carried, "col"), "row")
         block_rhs = lax.dynamic_index_in_dim(right_side, column, 1, keepdims=False).astype(
             jnp.float32
         )

time: 1430 us -> 1480 us (1.035)
  blocking collectives: 1280 us -> 1330 us
    psum x16 -> x32, blocking collectives: 643 us -> 696 us  [forward(): row_total = lax.psum(lax.psum(partial_value + carried, 'col'), 'row')]
where the time goes in v1:
time: 1480 us
  blocking collectives  1330 us (90%)
  matrix products  100 us (7%)
  local copies, waits for them, and re-layouts  33.4 us (2%)
    psum x32, blocking collectives, forward(): row_total = lax.psum(lax.psum(partial_value + carried, 'col'), 'row')  696 us
    psum x16, blocking collectives, backward(): col_total = lax.psum(partial_value, ('row', 'col'))  638 us

profile of v1, /device:TPU:0, one launch (start us, length us, event | category | flops | bytes accessed | tf_op | source)
XLA Modules:
  0.0 1475.4 jit_solution(7232808089595948276)
XLA Ops:
  5.8 768.7 %while.32 = (s32[]{:T(128)}, f32[8,16,512]{2,0,1:T(8,128)S(1)}, bf16[8,16,512]{2,1,0:T(8,128)(2,1)S(1)}, s32[2,4]{1,0:T(2,128)}, s32[]{:T(128)}, /*index=5*/bf16...) while((s32[]{:T(128)}, f32[8,16,512]{2,0,1:T(8,128)S(1)}, ...), condition=%wide.region_4.5_spmd.clone, body=%wide.region_1.4_spmd.clone.sunk | while | flops 33602120 | bytes 1851328 | solution.py:73
  21.7 37.4 %psum.49 = f32[8,512]{1,0:T(8,128)S(1)} all-reduce(f32[8,512]{1,0:T(8,128)S(1)} %psum.48), channel_id=1, replica_groups=mesh['row'=8,'col'=4] {'row'}, use_global_device_ids=true, to_apply=%region_3.3 | all-reduce | flops 4096 | bytes 32768 | tf_op jit(solution)/shard_map/while/body/eval_jaxpr/psum | solution.py:65
  121.4 33.0 %psum.49 = f32[8,512]{1,0:T(8,128)S(1)} all-reduce(f32[8,512]{1,0:T(8,128)S(1)} %psum.48), channel_id=1, replica_groups=mesh['row'=8,'col'=4] {'row'}, use_global_device_ids=true, to_apply=%region_3.3 | all-reduce | flops 4096 | bytes 32768 | tf_op jit(solution)/shard_map/while/body/eval_jaxpr/psum | solution.py:65
  169.0 33.0 %psum.49 = f32[8,512]{1,0:T(8,128)S(1)} all-reduce(f32[8,512]{1,0:T(8,128)S(1)} %psum.48), channel_id=1, replica_groups=mesh['row'=8,'col'=4] {'row'}, use_global_device_ids=true, to_apply=%region_3.3 | all-reduce | flops 4096 | bytes 32768 | tf_op jit(solution)/shard_map/while/body/eval_jaxpr/psum | solution.py:65
  216.6 33.0 %psum.49 = f32[8,512]{1,0:T(8,128)S(1)} all-reduce(f32[8,512]{1,0:T(8,128)S(1)} %psum.48), channel_id=1, replica_groups=mesh['row'=8,'col'=4] {'row'}, use_global_device_ids=true, to_apply=%region_3.3 | all-reduce | flops 4096 | bytes 32768 | tf_op jit(solution)/shard_map/while/body/eval_jaxpr/psum | solution.py:65
  264.2 33.0 %psum.49 = f32[8,512]{1,0:T(8,128)S(1)} all-reduce(f32[8,512]{1,0:T(8,128)S(1)} %psum.48), channel_id=1, replica_groups=mesh['row'=8,'col'=4] {'row'}, use_global_device_ids=true, to_apply=%region_3.3 | all-reduce | flops 4096 | bytes 32768 | tf_op jit(solution)/shard_map/while/body/eval_jaxpr/psum | solution.py:65
  359.4 33.0 %psum.49 = f32[8,512]{1,0:T(8,128)S(1)} all-reduce(f32[8,512]{1,0:T(8,128)S(1)} %psum.48), channel_id=1, replica_groups=mesh['row'=8,'col'=4] {'row'}, use_global_device_ids=true, to_apply=%region_3.3 | all-reduce | flops 4096 | bytes 32768 | tf_op jit(solution)/shard_map/while/body/eval_jaxpr/psum | solution.py:65
  775.3 697.6 %while.33 = (s32[]{:T(128)}, f32[8,16,512]{2,0,1:T(8,128)S(1)}, f32[8,16,512]{2,0,1:T(8,128)S(1)}, s32[2,4]{0,1:T(4,128)S(1)}, s32[]{:T(128)}, /*index=5*/bf16[2...) while((s32[]{:T(128)}, f32[8,16,512]{2,0,1:T(8,128)S(1)}, ...), condition=%wide.region_7.8_spmd.clone, body=%wide.region_5.7_spmd.clone.sunk | while | flops 29382456 | bytes 1203697 | solution.py:99
  777.5 36.9 %psum.50 = f32[8,512]{1,0:T(8,128)S(1)} all-reduce(f32[8,512]{1,0:T(8,128)S(1)} %fusion.113), channel_id=1, replica_groups=mesh['row'=8,'col'=4] {'row','col'}, use_global_device_ids=true, to_apply=%region_6.6 | all-reduce | flops 4096 | bytes 32768 | tf_op jit(solution)/shard_map/while/body/eval_jaxpr/psum | solution.py:93
  818.1 41.3 %psum.50 = f32[8,512]{1,0:T(8,128)S(1)} all-reduce(f32[8,512]{1,0:T(8,128)S(1)} %fusion.113), channel_id=1, replica_groups=mesh['row'=8,'col'=4] {'row','col'}, use_global_device_ids=true, to_apply=%region_6.6 | all-reduce | flops 4096 | bytes 32768 | tf_op jit(solution)/shard_map/while/body/eval_jaxpr/psum | solution.py:93
  863.0 39.5 %psum.50 = f32[8,512]{1,0:T(8,128)S(1)} all-reduce(f32[8,512]{1,0:T(8,128)S(1)} %fusion.113), channel_id=1, replica_groups=mesh['row'=8,'col'=4] {'row','col'}, use_global_device_ids=true, to_apply=%region_6.6 | all-reduce | flops 4096 | bytes 32768 | tf_op jit(solution)/shard_map/while/body/eval_jaxpr/psum | solution.py:93
  906.2 40.5 %psum.50 = f32[8,512]{1,0:T(8,128)S(1)} all-reduce(f32[8,512]{1,0:T(8,128)S(1)} %fusion.113), channel_id=1, replica_groups=mesh['row'=8,'col'=4] {'row','col'}, use_global_device_ids=true, to_apply=%region_6.6 | all-reduce | flops 4096 | bytes 32768 | tf_op jit(solution)/shard_map/while/body/eval_jaxpr/psum | solution.py:93
  950.4 39.5 %psum.50 = f32[8,512]{1,0:T(8,128)S(1)} all-reduce(f32[8,512]{1,0:T(8,128)S(1)} %fusion.113), channel_id=1, replica_groups=mesh['row'=8,'col'=4] {'row','col'}, use_global_device_ids=true, to_apply=%region_6.6 | all-reduce | flops 4096 | bytes 32768 | tf_op jit(solution)/shard_map/while/body/eval_jaxpr/psum | solution.py:93
  993.6 40.5 %psum.50 = f32[8,512]{1,0:T(8,128)S(1)} all-reduce(f32[8,512]{1,0:T(8,128)S(1)} %fusion.113), channel_id=1, replica_groups=mesh['row'=8,'col'=4] {'row','col'}, use_global_device_ids=true, to_apply=%region_6.6 | all-reduce | flops 4096 | bytes 32768 | tf_op jit(solution)/shard_map/while/body/eval_jaxpr/psum | solution.py:93
  1037.8 39.6 %psum.50 = f32[8,512]{1,0:T(8,128)S(1)} all-reduce(f32[8,512]{1,0:T(8,128)S(1)} %fusion.113), channel_id=1, replica_groups=mesh['row'=8,'col'=4] {'row','col'}, use_global_device_ids=true, to_apply=%region_6.6 | all-reduce | flops 4096 | bytes 32768 | tf_op jit(solution)/shard_map/while/body/eval_jaxpr/psum | solution.py:93
  1081.1 40.5 %psum.50 = f32[8,512]{1,0:T(8,128)S(1)} all-reduce(f32[8,512]{1,0:T(8,128)S(1)} %fusion.113), channel_id=1, replica_groups=mesh['row'=8,'col'=4] {'row','col'}, use_global_device_ids=true, to_apply=%region_6.6 | all-reduce | flops 4096 | bytes 32768 | tf_op jit(solution)/shard_map/while/body/eval_jaxpr/psum | solution.py:93
  1125.3 39.6 %psum.50 = f32[8,512]{1,0:T(8,128)S(1)} all-reduce(f32[8,512]{1,0:T(8,128)S(1)} %fusion.113), channel_id=1, replica_groups=mesh['row'=8,'col'=4] {'row','col'}, use_global_device_ids=true, to_apply=%region_6.6 | all-reduce | flops 4096 | bytes 32768 | tf_op jit(solution)/shard_map/while/body/eval_jaxpr/psum | solution.py:93
  1168.5 40.5 %psum.50 = f32[8,512]{1,0:T(8,128)S(1)} all-reduce(f32[8,512]{1,0:T(8,128)S(1)} %fusion.113), channel_id=1, replica_groups=mesh['row'=8,'col'=4] {'row','col'}, use_global_device_ids=true, to_apply=%region_6.6 | all-reduce | flops 4096 | bytes 32768 | tf_op jit(solution)/shard_map/while/body/eval_jaxpr/psum | solution.py:93
  1212.7 39.6 %psum.50 = f32[8,512]{1,0:T(8,128)S(1)} all-reduce(f32[8,512]{1,0:T(8,128)S(1)} %fusion.113), channel_id=1, replica_groups=mesh['row'=8,'col'=4] {'row','col'}, use_global_device_ids=true, to_apply=%region_6.6 | all-reduce | flops 4096 | bytes 32768 | tf_op jit(solution)/shard_map/while/body/eval_jaxpr/psum | solution.py:93
  1255.9 40.5 %psum.50 = f32[8,512]{1,0:T(8,128)S(1)} all-reduce(f32[8,512]{1,0:T(8,128)S(1)} %fusion.113), channel_id=1, replica_groups=mesh['row'=8,'col'=4] {'row','col'}, use_global_device_ids=true, to_apply=%region_6.6 | all-reduce | flops 4096 | bytes 32768 | tf_op jit(solution)/shard_map/while/body/eval_jaxpr/psum | solution.py:93
  1300.1 39.6 %psum.50 = f32[8,512]{1,0:T(8,128)S(1)} all-reduce(f32[8,512]{1,0:T(8,128)S(1)} %fusion.113), channel_id=1, replica_groups=mesh['row'=8,'col'=4] {'row','col'}, use_global_device_ids=true, to_apply=%region_6.6 | all-reduce | flops 4096 | bytes 32768 | tf_op jit(solution)/shard_map/while/body/eval_jaxpr/psum | solution.py:93
  1343.3 40.6 %psum.50 = f32[8,512]{1,0:T(8,128)S(1)} all-reduce(f32[8,512]{1,0:T(8,128)S(1)} %fusion.113), channel_id=1, replica_groups=mesh['row'=8,'col'=4] {'row','col'}, use_global_device_ids=true, to_apply=%region_6.6 | all-reduce | flops 4096 | bytes 32768 | tf_op jit(solution)/shard_map/while/body/eval_jaxpr/psum | solution.py:93
  1387.6 39.5 %psum.50 = f32[8,512]{1,0:T(8,128)S(1)} all-reduce(f32[8,512]{1,0:T(8,128)S(1)} %fusion.113), channel_id=1, replica_groups=mesh['row'=8,'col'=4] {'row','col'}, use_global_device_ids=true, to_apply=%region_6.6 | all-reduce | flops 4096 | bytes 32768 | tf_op jit(solution)/shard_map/while/body/eval_jaxpr/psum | solution.py:93
  1430.8 40.6 %psum.50 = f32[8,512]{1,0:T(8,128)S(1)} all-reduce(f32[8,512]{1,0:T(8,128)S(1)} %fusion.113), channel_id=1, replica_groups=mesh['row'=8,'col'=4] {'row','col'}, use_global_device_ids=true, to_apply=%region_6.6 | all-reduce | flops 4096 | bytes 32768 | tf_op jit(solution)/shard_map/while/body/eval_jaxpr/psum | solution.py:93
  (302 shorter events, 632.8 us)
Async XLA Ops:
  0.6 1473.8 %copy-start = (bf16[1,512,512]{2,1,0:T(8,128)(2,1)S(1)}, bf16[1,512,512]{2,1,0:T(8,128)(2,1)}, u32[]{:S(2)}) copy-start(bf16[1,512,512]{2,1,0:T(8,128)(2,1)} %param.20) | copy-start | bytes 1572868
  5.7 1468.4 %copy-start.1 = (bf16[1,512,1024]{2,1,0:T(8,128)(2,1)S(1)}, bf16[1,512,1024]{2,1,0:T(8,128)(2,1)}, u32[]{:S(2)}) copy-start(bf16[1,512,1024]{2,1,0:T(8,128)(2,1)} %param.19) | copy-start | bytes 3145732
  5.8 1468.7 %copy-start.2 = (bf16[1,8,512]{2,1,0:T(8,128)(2,1)S(1)}, bf16[1,8,512]{2,1,0:T(8,128)(2,1)}, u32[]{:S(2)}) copy-start(bf16[1,8,512]{2,1,0:T(8,128)(2,1)} %param.18) | copy-start | bytes 24580
